TPU v7x, 32 devices: a whole 2x2x4 slice. The times are simulated.
32 devices in a mesh: img: 2 (over x), ga: 4 (over y, core), band: 4 (over z).
Axes of the slice: x: 2, y: 2, z: 4, core: 2. Of those that a mesh axis runs over, the one named last changes fastest.
Arguments:
- orbitals: bfloat16 [1536, 12288], P(('img', 'band'), 'ga'), parts along dimension 0, as said below
- kernel: float32 [12288], P('ga'), may hold values from 0.3 to 3
- block_vectors: bfloat16 [512, 12288], P(('img', 'band'), 'ga'), parts along dimension 0
Outputs:
- ace_vectors: bfloat16 [1536, 12288], P(('img', 'band'), 'ga'), parts along dimension 0
- exchange_block: bfloat16 [512, 12288], P(('img', 'band'), 'ga'), parts along dimension 0
There are 2 independent parts, one for each index of `img`. A program takes and returns all parts, laid end to end along the dimension named above; an argument that names none is the same for every part. Nothing has to cross between parts.
Inputs may be any that keep to these rules, and one draw needn't show every extreme that they name: `orbitals`: the bands of one image are linearly independent, and the block lies largely in their span.
All inputs are finite; a program needn't handle non-finite values.
Results may differ from a plain program's by a relative error of at most 0.02.
Values may be sent and summed in bfloat16 or wider, within the bound.
A program may use at most 64 MiB of HBM per device.

v0:
```python
import jax
import jax.numpy as jnp
from jax import lax
from jax.sharding import PartitionSpec as P


def contract_first(left, right):
    return lax.dot_general(left, right, (((0,), (0,)), ((), ())), precision=lax.Precision.HIGHEST)


def shards(orbitals, kernel, block_vectors):
    groups = lax.axis_size("ga")
    own_band = lax.axis_index("band")
    total_coeffs = orbitals.shape[1] * groups
    full_orbitals, full_block = (
        lax.all_gather(orbitals, "band", axis=0, tiled=True),
        lax.all_gather(block_vectors, "band", axis=0, tiled=True),
    )
    weighted = (-(full_orbitals.astype(jnp.float32) * kernel[None, :])).astype(jnp.bfloat16)
    own_rows = orbitals.shape[0]
    partial_rows = lax.dot_general(
        orbitals, weighted, (((1,), (1,)), ((), ())), preferred_element_type=jnp.float32
    )
    summed_rows = lax.psum(partial_rows.astype(jnp.bfloat16), "ga").astype(jnp.float32)
    margin = -lax.all_gather(summed_rows, "band", axis=0, tiled=True) / total_coeffs
    factor = jnp.linalg.cholesky(margin)
    identity = jnp.eye(factor.shape[0], dtype=jnp.float32)
    inverse = lax.linalg.triangular_solve(factor, identity, left_side=True, lower=True)
    inverse_rows = lax.dynamic_slice_in_dim(inverse, own_band * own_rows, own_rows, 0)
    projector = jnp.dot(inverse_rows, weighted.astype(jnp.float32), precision=lax.Precision.HIGHEST)
    local_coupling = jnp.dot(
        projector, full_block.astype(jnp.float32).T, precision=lax.Precision.HIGHEST
    )
    coupling = (
        lax.psum(local_coupling.astype(jnp.bfloat16), "ga").astype(jnp.float32) / total_coeffs
    )
    applied = lax.psum_scatter(
        -contract_first(coupling, projector), "band", scatter_dimension=0, tiled=True
    )
    return (projector.astype(jnp.bfloat16), applied.astype(jnp.bfloat16))


def solution(mesh):
    placed = (P(("img", "band"), "ga"), P("ga"), P(("img", "band"), "ga"))
    return jax.shard_map(
        shards,
        mesh=mesh,
        in_specs=placed,
        out_specs=(P(("img", "band"), "ga"), P(("img", "band"), "ga")),
        check_vma=False,
    )
```

profile of v0, /device:TPU:25, one launch (start us, length us, event | category | flops | bytes accessed | tf_op | source)
XLA Modules:
  0.0 545.9 jit_solution(6717364289099904385)
XLA Ops:
  7.9 89.3 %all-gather.4.cloned.1.call-done = bf16[768,3072]{1,0:T(8,128)(2,1)} async-done(((bf16[192,3072]{1,0:T(8,128)(2,1)}), bf16[768,3072]{1,0:T(8,128)(2,1)}) %all-gather.4.cloned.1.call-update) | async-done | bytes 4718608 | tf_op jit(solution)/shard_map/all_gather | solution.py:16
  97.3 5.1 fusion.20
  102.5 32.5 %all-reduce.4.cloned.1.call-done = bf16[192,768]{1,0:T(8,128)(2,1)} async-done(((bf16[192,768]{1,0:T(8,128)(2,1)}), bf16[192,768]{1,0:T(8,128)(2,1)}) %all-reduce.4.cloned.1.call-update) | async-done | bytes 294928 | tf_op jit(solution)/shard_map/psum | solution.py:24
  135.0 1.8 convert_element_type.44
  137.7 1.6 fusion.24
  139.3 47.2 %all-gather.6.cloned.1.call-done = f32[768,768]{1,0:T(8,128)} async-done(((f32[192,768]{1,0:T(8,128)}), f32[768,768]{1,0:T(8,128)}) %all-gather.6.cloned.1.call-update) | async-done | bytes 2359312 | tf_op jit(solution)/shard_map/all_gather | solution.py:25
  186.5 2.0 copy.7
  188.5 1.7 negate_multiply_fusion
  190.2 3.6 copy.8
  193.8 2.0 fusion.2
  195.8 1.5 copy-done.1
  197.2 11.7 %cholesky.165 = f32[128,128]{1,0:T(8,128)S(1)} custom-call(f32[128,128]{1,0:T(8,128)S(1)} %cholesky.424), custom_call_target="Cholesky" | custom-call | tf_op jit(solution)/shard_map/jit(cholesky)/cholesky | solution.py:26
  209.0 9.8 %custom-call.46 = f32[1,128,128]{1,2,0:T(8,128)S(1)} custom-call(f32[1,128,128]{2,1,0:T(8,128)S(1)} %get-tuple-element.45), custom_call_target="InvertDiagBlocksLowerTriangular" | custom-call | tf_op jit(solution)/shard_map/jit(cholesky)/cholesky | solution.py:26
  219.0 1.4 constant_dynamic-update-slice_fusion.15
  220.3 1.4 convolution_subtract_fusion.4
  221.8 11.7 %cholesky.188 = f32[128,128]{1,0:T(8,128)S(1)} custom-call(f32[128,128]{1,0:T(8,128)S(1)} %cholesky.428), custom_call_target="Cholesky" | custom-call | tf_op jit(solution)/shard_map/jit(cholesky)/cholesky | solution.py:26
  233.5 10.0 %custom-call.47 = f32[1,128,128]{1,2,0:T(8,128)S(1)} custom-call(f32[1,128,128]{2,1,0:T(8,128)S(1)} %get-tuple-element.42), custom_call_target="InvertDiagBlocksLowerTriangular" | custom-call | tf_op jit(solution)/shard_map/jit(cholesky)/cholesky | solution.py:26
  243.9 1.5 convolution_subtract_fusion.5
  245.4 11.7 %cholesky.354 = f32[128,128]{1,0:T(8,128)S(1)} custom-call(f32[128,128]{1,0:T(8,128)S(1)} %cholesky.433), custom_call_target="Cholesky" | custom-call | tf_op jit(solution)/shard_map/jit(cholesky)/cholesky | solution.py:26
  257.8 9.8 %custom-call.48 = f32[1,128,128]{1,2,0:T(8,128)S(1)} custom-call(f32[1,128,128]{2,1,0:T(8,128)S(1)} %get-tuple-element.39), custom_call_target="InvertDiagBlocksLowerTriangular" | custom-call | tf_op jit(solution)/shard_map/jit(cholesky)/cholesky | solution.py:26
  268.0 1.6 convolution_subtract_fusion.6
  269.6 12.1 %cholesky.373 = f32[128,128]{1,0:T(8,128)S(1)} custom-call(f32[128,128]{1,0:T(8,128)S(1)} %cholesky.438), custom_call_target="Cholesky" | custom-call | tf_op jit(solution)/shard_map/jit(cholesky)/cholesky | solution.py:26
  282.4 9.8 %custom-call.49 = f32[1,128,128]{1,2,0:T(8,128)S(1)} custom-call(f32[1,128,128]{2,1,0:T(8,128)S(1)} %get-tuple-element.36), custom_call_target="InvertDiagBlocksLowerTriangular" | custom-call | tf_op jit(solution)/shard_map/jit(cholesky)/cholesky | solution.py:26
  292.5 1.5 convolution_subtract_fusion.7
  294.0 11.7 %cholesky.392 = f32[128,128]{1,0:T(8,128)S(1)} custom-call(f32[128,128]{1,0:T(8,128)S(1)} %cholesky.443), custom_call_target="Cholesky" | custom-call | tf_op jit(solution)/shard_map/jit(cholesky)/cholesky | solution.py:26
  306.5 9.8 %custom-call.50 = f32[1,128,128]{1,2,0:T(8,128)S(1)} custom-call(f32[1,128,128]{2,1,0:T(8,128)S(1)} %get-tuple-element.33), custom_call_target="InvertDiagBlocksLowerTriangular" | custom-call | tf_op jit(solution)/shard_map/jit(cholesky)/cholesky | solution.py:26
  316.5 1.3 convolution_subtract_fusion.8
  317.8 11.9 %cholesky.410 = f32[128,128]{1,0:T(8,128)S(1)} custom-call(f32[128,128]{1,0:T(8,128)S(1)} %convolution_subtract_fusion.8), custom_call_target="Cholesky" | custom-call | tf_op jit(solution)/shard_map/jit(cholesky)/cholesky | solution.py:26
  335.0 1.6 select_select_fusion
  336.6 21.3 %while.1 = (s32[]{:T(128)}, f32[768,768]{1,0:T(8,128)}, s32[6,2]{0,1:T(2,128)S(1)}, f32[6,128,128]{2,1,0:T(8,128)}, s32[]{:T(128)}) while((s32[]{:T(128)}, f32[768,768]{1,0:T(8,128)}, s32[6,2]{0,1:T(2,128)S(1)}, f32[6,128,128]{2,1,0:T(8,128)}, s32[]{:T(128)}) %tuple.45), condition=%wide.while_cond, body=%wide.while_body.sunk | while | flops 2 | bytes 132705 | solution.py:28
  337.3 3.0 bitcast_dynamic-update-slice_fusion.2
  340.9 2.9 bitcast_dynamic-update-slice_fusion.2
  344.4 2.9 bitcast_dynamic-update-slice_fusion.2
  348.0 2.9 bitcast_dynamic-update-slice_fusion.2
  351.5 2.9 bitcast_dynamic-update-slice_fusion.2
  355.1 2.8 bitcast_dynamic-update-slice_fusion.2
  357.9 60.4 %custom-call.51 = f32[6,128,128]{1,2,0:T(8,128)} custom-call(f32[6,128,128]{2,1,0:T(8,128)} %get-tuple-element.9), custom_call_target="InvertDiagBlocksLowerTriangular" | custom-call | tf_op jit(solution)/shard_map/triangular_solve | solution.py:28
  419.6 1.5 convolution_subtract_fusion.2
  421.7 1.5 convolution_subtract_fusion.3
  423.7 2.0 convolution_subtract_fusion.1
  426.2 2.0 fusion.12
  428.8 2.3 convolution_subtract_fusion
  431.6 4.2 fusion.65
  435.9 3.8 convolution_convert_fusion
  440.0 31.1 %all-reduce.6.cloned.1.call-done = bf16[192,256]{1,0:T(8,128)(2,1)} async-done(((bf16[192,256]{1,0:T(8,128)(2,1)}), bf16[192,256]{1,0:T(8,128)(2,1)}) %all-reduce.6.cloned.1.call-update) | async-done | bytes 98320 | tf_op jit(solution)/shard_map/psum | solution.py:35
  471.1 5.3 convolution_negate_fusion
  476.5 60.5 %reduce-scatter.2.cloned.1.call-done = f32[64,3072]{1,0:T(8,128)} async-done(((f32[256,3072]{1,0:T(8,128)}), f32[64,3072]{1,0:T(8,128)}) %reduce-scatter.2.cloned.1.call-update) | async-done | bytes 786448 | tf_op jit(solution)/shard_map/reduce_scatter | solution.py:37
  536.9 1.9 convert_element_type.49
  (68 shorter events, 14.7 us)
Async XLA Ops:
  7.2 90.1 %all-gather.4.cloned.1.call-start = ((), (), s32[]{:S(2)}) async-start(), calls=%async_computation.1 | async-start | bytes 5898240 | tf_op jit(solution)/shard_map/all_gather | solution.py:16
  7.9 127.1 %all-reduce.4.cloned.1.call-start = ((), (), s32[]{:S(2)}) async-start(), calls=%async_computation.2 | async-start | bytes 589824 | tf_op jit(solution)/shard_map/psum | solution.py:24
  102.5 84.0 %all-gather.6.cloned.1.call-start = ((), (), s32[]{:S(2)}) async-start(), calls=%async_computation.3 | async-start | bytes 2949120 | tf_op jit(solution)/shard_map/all_gather | solution.py:25
  136.9 299.0 %all-gather.8.cloned.1.call-start = ((), (), s32[]{:S(2)}) async-start(), calls=%async_computation.4 | async-start | bytes 1966080 | tf_op jit(solution)/shard_map/all_gather | solution.py:17
  137.5 333.7 %all-reduce.6.cloned.1.call-start = ((), (), s32[]{:S(2)}) async-start(), calls=%async_computation.5 | async-start | bytes 196608 | tf_op jit(solution)/shard_map/psum | solution.py:35
  195.8 1.5 copy-start.1
  336.6 85.0 %copy-start = (f32[768,768]{1,0:T(8,128)S(1)}, f32[768,768]{1,0:T(8,128)}, u32[]{:S(2)}) copy-start(f32[768,768]{1,0:T(8,128)} %fusion.24) | copy-start | bytes 7077892
  418.3 2.8 copy-start.2
  423.7 7.9 %slice-start = ((s8[4718592]{0:T(1024)(128)(4,1)}), s8[4194304]{0:T(1024)(128)(4,1)S(1)}, s32[]{:S(2)}) async-start(s8[4718592]{0:T(1024)(128)(4,1)} %bitcast.83), calls=%async_computation.7 | async-start | bytes 8388608
  426.2 5.4 slice-start.1
  428.2 3.4 copy-start.3
  439.7 97.2 %reduce-scatter.2.cloned.1.call-start = ((), (), s32[]{:S(2)}) async-start(), calls=%async_computation.6 | async-start | bytes 3932160 | tf_op jit(solution)/shard_map/reduce_scatter | solution.py:37
Sparse Core Ops, SparseCore 0:
  9.5 87.7 all-gather.3
  102.6 32.4 all-reduce.3
  137.2 49.2 all-gather.5
  187.9 35.4 all-gather.7
  439.8 31.2 all-reduce.5
  476.6 60.3 reduce-scatter.1
where the time goes:
time: 553 us; the launch traced here: 546 us
  waiting for transfers between devices  262 us (47%)
  other arithmetic  195 us (35%)
  matrix products  41.5 us (8%)
  local copies, waits for them, and re-layouts  28.5 us (5%)
  between operations  18.6 us (3%)
    another operation x22, other arithmetic, shards(): factor = jnp.linalg.cholesky(margin)  124 us
    all_gather x1, waiting for transfers between devices, shards(): lax.all_gather(orbitals, 'band', axis=0, tiled=True)  89.3 us
    another operation x3, other arithmetic, shards(): lax.linalg.triangular_solve(factor, identity, left_side=True, lower=True)  62 us
    reduce_scatter x1, waiting for transfers between devices, shards(): lax.psum_scatter(-contract_first(coupling, projector), 'band', scatter_di...  60.5 us
    all_gather x1, waiting for transfers between devices, shards(): lax.all_gather(summed_rows, 'band', axis=0, tiled=True)  47.2 us
    psum x1, waiting for transfers between devices, shards(): lax.psum(partial_rows.astype(jnp.bfloat16), 'ga').astype(jnp.float32)  32.5 us
    psum x1, waiting for transfers between devices, shards(): lax.psum(local_coupling.astype(jnp.bfloat16), 'ga').astype(jnp.float32)  31.1 us
    another operation x18, local copies, waits for them, and re-layouts  21.3 us
  transfers between devices with their start and end apart: 6, of which 5 were waited for; matrix products, arithmetic and copies ran while one was open for 45% of the time, Pallas kernels for 0%

commit v1 on v0

v1 whole, which is shorter than its diff:
```python
import functools

import jax
import jax.numpy as jnp
from jax import lax
from jax.experimental import pallas as pl
from jax.experimental.pallas import tpu as pltpu
from jax.sharding import PartitionSpec as P

MESH = pl.DeviceIdType.MESH
F32 = jnp.float32
BF16 = jnp.bfloat16
TILE = 128


def send(src, dst, send_sem, recv_sem, where):
    copy = pltpu.make_async_remote_copy(
        src_ref=src, dst_ref=dst, send_sem=send_sem, recv_sem=recv_sem,
        device_id=where, device_id_type=MESH,
    )
    copy.start()
    return copy


def greet(places):
    barrier = pltpu.get_barrier_semaphore()
    for place in places:
        pl.semaphore_signal(barrier, inc=1, device_id=place, device_id_type=MESH)
    pl.semaphore_wait(barrier, len(places))


def dot(a, b, dims):
    return lax.dot_general(a, b, (dims, ((), ())), preferred_element_type=F32)


def margin_kernel(bands, groups, orb, kern, blk, m_out, s_out, w_out,
                  full, part32, part16, rx_core, acc, out_z, rx_z, out_y, rx_y, allg,
                  a_s, a_r, b_s, b_r, loc, c_s, c_r, z_s, z_r, y_s, y_r, g_s, g_r, f_s, f_r):
    me = lax.axis_index("band")
    ga = lax.axis_index("ga")
    own, bown = orb.shape[0], blk.shape[0]
    cols = orb.shape[1] // bands
    n = own * bands
    half = full.shape[0] // 2
    total = orb.shape[1] * groups
    core = lax.rem(ga, 2)
    partner = {"ga": ga + 1 - 2 * core}
    peer = [lax.rem(me + d, bands) for d in range(bands)]
    order = sorted(range(1, bands), key=lambda d: -min(d, bands - d))
    bits = []
    stride = 2
    while stride < groups:
        bits.append({"ga": ga + stride * (1 - 2 * lax.rem(ga // stride, 2))})
        stride *= 2
    greet([{"band": peer[d]} for d in range(1, bands)] + [partner] + bits)

    def chunk(d):
        return pl.ds(pl.multiple_of(peer[d] * cols, TILE), cols)

    mine = pl.ds(pl.multiple_of(me * own, 16), own)
    mine_b = pl.ds(pl.multiple_of(n + me * bown, 16), bown)
    local_a = pltpu.make_async_copy(orb.at[:, chunk(0)], full.at[mine], loc.at[0])
    local_a.start()
    local_b = pltpu.make_async_copy(blk.at[:, chunk(0)], full.at[mine_b], loc.at[1])
    local_b.start()
    copies_a = [send(orb.at[:, chunk(d)], full.at[mine], a_s.at[d], a_r.at[d], {"band": peer[d]})
                for d in order]
    copies_b = [send(blk.at[:, chunk(d)], full.at[mine_b], b_s.at[d], b_r.at[d], {"band": peer[d]})
                for d in order]
    local_a.wait()
    local_b.wait()
    for copy in copies_a:
        copy.wait()
    w_out[...] = (-(full[0:n, :].astype(F32) * kern[:, chunk(0)])).astype(BF16)
    for copy in copies_b:
        copy.wait()
    for h in range(2):
        product = dot(w_out[...], full[h * half:(h + 1) * half, :], ((1,), (1,)))
        part32[h] = product
        part16[h] = product.astype(BF16)
    send(part16.at[1 - core], rx_core, c_s, c_r, partner).wait()
    acc[...] = part32[core] + rx_core[...].astype(F32)
    out_z[...] = acc[...].astype(BF16)
    copies = [send(out_z.at[pl.ds(pl.multiple_of(peer[d] * own, 16), own)], rx_z.at[d],
                   z_s.at[d], z_r.at[d], {"band": peer[d]}) for d in order]
    for copy in copies:
        copy.wait()
    total_rows = acc[mine, :]
    for d in range(1, bands):
        total_rows = total_rows + rx_z[d].astype(F32)
    for i, place in enumerate(bits):
        out_y[i] = total_rows.astype(BF16)
        send(out_y.at[i], rx_y.at[i], y_s.at[i], y_r.at[i], place).wait()
        total_rows = out_y[i].astype(F32) + rx_y[i].astype(F32)
    allg[core, mine, :] = total_rows.astype(BF16)
    block = allg.at[core, mine]
    copies = {d: send(block, block, g_s.at[d], g_r.at[d], {"band": peer[d]}) for d in order}
    forwards = [send(block, block, f_s.at[0], f_r.at[0], partner)]
    for d in sorted(range(1, bands), key=lambda d: min(d, bands - d)):
        copies[d].wait()
        source = lax.rem(me + bands - d, bands)
        there = allg.at[core, pl.ds(pl.multiple_of(source * own, 16), own)]
        forwards.append(send(there, there, f_s.at[d], f_r.at[d], partner))
    for copy in forwards:
        copy.wait()
    scale = 1.0 / total
    m_out[:, 0:half] = allg[0].astype(F32) * -scale
    m_out[:, half:n] = allg[1, :, 0:n - half].astype(F32) * -scale
    s_out[...] = (allg[1, :, n - half:].astype(F32) * scale).astype(BF16)


def split(a):
    high = a.astype(BF16)
    return high, (a - high.astype(F32)).astype(BF16)


def product3(a, b, dims):
    (ah, al), (bh, bl) = split(a), split(b)
    return dot(ah, bh, dims) + (dot(ah, bl, dims) + dot(al, bh, dims))


def identity(rows):
    shape = (rows, rows)
    return (lax.broadcasted_iota(jnp.int32, shape, 0)
            == lax.broadcasted_iota(jnp.int32, shape, 1)).astype(F32)


def factor_tile(d_ref, t_ref):
    G = 8
    sub = lax.broadcasted_iota(jnp.int32, (G, TILE), 0)

    def spread(row):
        return jnp.broadcast_to(row, (G, TILE))

    def step(g, carry):
        start = pl.multiple_of(g * G, G)
        left = d_ref[pl.ds(start, G), 0:TILE]
        right = d_ref[pl.ds(start, G), TILE:2 * TILE]
        turned = pltpu.roll(left, lax.rem(TILE - start, TILE), 1)
        columns = [jnp.broadcast_to(turned[:, c:c + 1], (G, TILE)) for c in range(G)]
        d = [[spread(columns[c][i:i + 1, :]) for c in range(i + 1)] for i in range(G)]
        u, v = [], []
        u_all = v_all = jnp.zeros((G, TILE), F32)
        for j in range(G):
            r = lax.rsqrt(d[j][j])
            for i in range(j + 1, G):
                d[i][j] = d[i][j] * r
            for i in range(j + 1, G):
                for c in range(j + 1, i + 1):
                    d[i][c] = d[i][c] - d[i][j] * d[c][j]
            a, b = spread(left[j:j + 1, :]), spread(right[j:j + 1, :])
            for t in range(j):
                a = a - d[j][t] * u[t]
                b = b - d[j][t] * v[t]
            u.append(a * r)
            v.append(b * r)
            u_all = jnp.where(sub == j, u[j], u_all)
            v_all = jnp.where(sub == j, v[j], v_all)
        t_ref[pl.ds(start, G), :] = v_all
        both = jnp.concatenate([u_all, v_all], axis=1)
        high = both.astype(BF16).astype(F32)
        low = both - high
        lhs = jnp.concatenate([high[:, :TILE], high[:, :TILE], low[:, :TILE], low[:, :TILE]], axis=0)
        rhs = jnp.concatenate([high, low, high, low], axis=0)
        d_ref[...] -= dot(lhs.astype(BF16), rhs.astype(BF16), ((0,), (0,)))
        return carry

    lax.fori_loop(0, TILE // G, step, 0)


def factor_kernel(m_ref, x_ref, a, rest, d_ref, t_ref):
    n = m_ref.shape[0]
    a[...] = m_ref[...]
    rest[...] = identity(n)
    x_ref[...] = jnp.zeros_like(x_ref)
    for s in range(0, n, TILE):
        e = s + TILE
        d_ref[:, 0:TILE] = a[s:e, s:e]
        d_ref[:, TILE:] = identity(TILE)
        factor_tile(d_ref, t_ref)
        tile = t_ref[...]
        rows = product3(tile, rest[s:e, 0:e], ((1,), (0,)))
        x_ref[s:e, 0:e] = rows.astype(BF16)
        if e < n:
            panel = product3(a[e:, s:e], tile, ((1,), (1,)))
            a[e:, e:] -= product3(panel, panel, ((1,), (1,)))
            rest[e:, 0:e] -= product3(panel, rows, ((1,), (0,)))


def apply_kernel(bands, x, s, w, ace, exch, proj, applied, p_s, p_r, e_s, e_r, loc):
    me = lax.axis_index("band")
    own, bown = ace.shape[0], exch.shape[0]
    cols = w.shape[1]
    peer = [lax.rem(me + d, bands) for d in range(bands)]
    order = sorted(range(1, bands), key=lambda d: -min(d, bands - d))
    greet([{"band": peer[d]} for d in range(1, bands)])
    here = pl.ds(pl.multiple_of(me * cols, TILE), cols)
    copies = []
    for d in order + [0]:
        rows = pl.ds(pl.multiple_of(peer[d] * own, 16), own)
        proj[rows, :] = dot(x[rows, :], w[...], ((1,), (0,))).astype(BF16)
        if d:
            copies.append(send(proj.at[rows], ace.at[:, here], p_s.at[d], p_r.at[d], {"band": peer[d]}))
        else:
            copies.append(pltpu.make_async_copy(proj.at[rows], ace.at[:, here], loc.at[0]))
            copies[-1].start()
    coupling = dot(x[...], s[...], ((1,), (0,))).astype(BF16)
    applied[...] = (-dot(coupling, proj[...], ((0,), (0,)))).astype(BF16)
    for d in order + [0]:
        rows = pl.ds(pl.multiple_of(peer[d] * bown, 16), bown)
        if d:
            copies.append(send(applied.at[rows], exch.at[:, here], e_s.at[d], e_r.at[d], {"band": peer[d]}))
        else:
            copies.append(pltpu.make_async_copy(applied.at[rows], exch.at[:, here], loc.at[1]))
            copies[-1].start()
    for copy in copies:
        copy.wait()


def shards(orbitals, kernel, block_vectors):
    groups, bands = lax.axis_size("ga"), lax.axis_size("band")
    own, width = orbitals.shape
    bown = block_vectors.shape[0]
    cols = width // bands
    n, nblk = own * bands, bown * bands
    half = (n + nblk) // 2
    levels = max(groups.bit_length() - 2, 1)
    vmem, hbm = pl.BlockSpec(memory_space=pltpu.VMEM), pl.BlockSpec(memory_space=pl.ANY)
    dma = pltpu.SemaphoreType.DMA
    many = dma((bands,))
    margin, s, weighted = pl.pallas_call(
        functools.partial(margin_kernel, bands, groups),
        name="margin",
        out_shape=(
            jax.ShapeDtypeStruct((n, n), F32),
            jax.ShapeDtypeStruct((n, nblk), BF16),
            jax.ShapeDtypeStruct((n, cols), BF16),
        ),
        in_specs=[hbm, vmem, hbm],
        out_specs=(vmem, vmem, vmem),
        scratch_shapes=[
            pltpu.VMEM((n + nblk, cols), BF16),
            pltpu.VMEM((2, n, half), F32),
            pltpu.VMEM((2, n, half), BF16),
            pltpu.VMEM((n, half), BF16),
            pltpu.VMEM((n, half), F32),
            pltpu.VMEM((n, half), BF16),
            pltpu.VMEM((bands, own, half), BF16),
            pltpu.VMEM((levels, own, half), BF16),
            pltpu.VMEM((levels, own, half), BF16),
            pltpu.VMEM((2, n, half), BF16),
            many, many, many, many, dma((2,)), dma, dma, many, many,
            dma((levels,)), dma((levels,)), many, many, many, many,
        ],
        compiler_params=pltpu.CompilerParams(
            collective_id=0, has_side_effects=True, vmem_limit_bytes=48 * 2**20),
    )(orbitals, kernel.reshape(1, width), block_vectors)
    inverse = pl.pallas_call(
        factor_kernel,
        name="factor",
        out_shape=jax.ShapeDtypeStruct((n, n), BF16),
        in_specs=[vmem],
        out_specs=vmem,
        scratch_shapes=[
            pltpu.VMEM((n, n), F32),
            pltpu.VMEM((n, n), F32),
            pltpu.VMEM((TILE, 2 * TILE), F32),
            pltpu.VMEM((TILE, TILE), F32),
        ],
        compiler_params=pltpu.CompilerParams(vmem_limit_bytes=48 * 2**20),
    )(margin)
    return pl.pallas_call(
        functools.partial(apply_kernel, bands),
        name="apply",
        out_shape=(
            jax.ShapeDtypeStruct((own, width), BF16),
            jax.ShapeDtypeStruct((bown, width), BF16),
        ),
        in_specs=[vmem, vmem, vmem],
        out_specs=(hbm, hbm),
        scratch_shapes=[
            pltpu.VMEM((n, cols), BF16),
            pltpu.VMEM((nblk, cols), BF16),
            many, many, many, many, dma((2,)),
        ],
        compiler_params=pltpu.CompilerParams(
            collective_id=1, has_side_effects=True, vmem_limit_bytes=48 * 2**20),
    )(inverse, s, weighted)


def solution(mesh):
    placed = (P(("img", "band"), "ga"), P("ga"), P(("img", "band"), "ga"))
    return jax.shard_map(
        shards,
        mesh=mesh,
        in_specs=placed,
        out_specs=(P(("img", "band"), "ga"), P(("img", "band"), "ga")),
        check_vma=False,
    )
```

time: 553 us -> 176 us (0.32)
  waiting for transfers between devices: 262 us -> 0 us
  other arithmetic: 195 us -> 0 us
  Pallas kernels: 0 us -> 167 us
  matrix products: 41.5 us -> 0 us
  local copies, waits for them, and re-layouts: 28.5 us -> 4.73 us
  between operations: 18.6 us -> 0.66 us
    another operation x25 -> x0, other arithmetic: 186 us -> none  [the longest x22 124 us: shards(): factor = jnp.linalg.cholesky(margin)]
    pallas_call x0 -> x3, Pallas kernels: none -> 167 us  [the longest x1 81.9 us: shards(): pl.pallas_call(functools.partial(margin_kernel, bands, groups), name='mar...]
    all_gather x3 -> x0, waiting for transfers between devices: 137 us -> none  [the longest x1 89.3 us: shards(): lax.all_gather(orbitals, 'band', axis=0, tiled=True)]
    psum x2 -> x0, waiting for transfers between devices: 63.7 us -> none  [the longest x1 32.5 us: shards(): lax.psum(partial_rows.astype(jnp.bfloat16), 'ga').astype(jnp.float32)]
    reduce_scatter x1 -> x0, waiting for transfers between devices: 60.5 us -> none  [shards(): lax.psum_scatter(-contract_first(coupling, projector), 'band', scatter_di...]
    another operation x21 -> x0, matrix products: 23 us -> none  [the longest x11 13.2 us: shards(): lax.linalg.triangular_solve(factor, identity, left_side=True, lower=True)]
    another operation x25 -> x0, local copies, waits for them, and re-layouts: 21.5 us -> none
    dot_general x4 -> x0, matrix products: 18.5 us -> none  [the longest x1 5.31 us: contract_first(): lax.dot_general(left, right, (((0,), (0,)), ((), ())), precision=lax.Prec...]
  transfers between devices with their start and end apart: 6 -> 0, of which waited for: 5 -> 0; matrix products, arithmetic and copies ran while one was open for 45% -> 0% of each run, Pallas kernels for 0% -> 0%
where the time goes in v1:
time: 176 us; the launch traced here: 172 us
  Pallas kernels  167 us (95%)
  local copies, waits for them, and re-layouts  4.73 us (3%)
    pallas_call x1, Pallas kernels, shards(): pl.pallas_call(functools.partial(margin_kernel, bands, groups), name='mar...  81.9 us
    pallas_call x1, Pallas kernels, shards(): pl.pallas_call(factor_kernel, name='factor', out_shape=jax.ShapeDtypeStru...  48 us
    pallas_call x1, Pallas kernels, shards(): pl.pallas_call(functools.partial(apply_kernel, bands), name='apply', out_...  36.9 us
    unnamed x8, local copies, waits for them, and re-layouts  4.73 us

profile of v1, /device:TPU:25, one launch (start us, length us, event | category | flops | bytes accessed | tf_op | source)
XLA Modules:
  0.0 172.2 jit_solution(11228540869300624426)
XLA Ops:
  0.6 0.0 copy-start
  0.6 1.3 copy-done
  1.9 0.0 copy-start.1
  1.9 1.0 copy-done.1
  2.9 0.0 copy-start.2
  2.9 0.7 copy-done.2
  3.6 81.9 %margin.1 = (f32[768,768]{1,0:T(8,128)S(1)}, bf16[768,256]{1,0:T(8,128)(2,1)S(1)}, bf16[768,768]{1,0:T(8,128)(2,1)S(1)}) custom-call(bf16[192,3072]{1,0:T(8,128)(2,1)S(1)} %copy-done, f32[1,3072]{1,0:T(1,128)S(1)} %bitcast.1, bf16[64,3072]{1,0:T(8,128)(2,1)S(1)} %copy-done.1), custom_call_target="tpu_custom_call" | custom-call | tf_op jit(solution)/shard_map/margin/pallas_call | solution.py:231
  85.5 48.0 %factor.1.x = bf16[768,768]{1,0:T(8,128)(2,1)S(1)} custom-call(f32[768,768]{1,0:T(8,128)S(1)} %get-tuple-element.5.m_ref), custom_call_target="tpu_custom_call" | custom-call | tf_op jit(solution)/shard_map/factor/pallas_call | solution.py:258
  133.6 36.9 %apply.1 = (bf16[192,3072]{1,0:T(8,128)(2,1)S(1)}, bf16[64,3072]{1,0:T(8,128)(2,1)S(1)}) custom-call(bf16[768,768]{1,0:T(8,128)(2,1)S(1)} %factor.1.x, bf16[768,256]{1,0:T(8,128)(2,1)S(1)} %get-tuple-element.6.s, bf16[768,768]{1,0:T(8,128)(2,1)S(1)} %get-tuple-element.7.w), custom_call_target="tpu_custom_call" | custom-call | tf_op jit(solution)/shard_map/apply/pallas_call | solution.py:272
  170.5 1.0 copy.7
  171.5 0.7 copy.8
Async XLA Ops:
  0.6 1.3 copy-start
  1.9 1.0 copy-start.1
  2.9 0.7 copy-start.2

commit v2 on v0

v2 whole, which is shorter than its diff:
```python
import functools

import jax
import jax.numpy as jnp
from jax import lax
from jax.experimental import pallas as pl
from jax.experimental.pallas import tpu as pltpu
from jax.sharding import PartitionSpec as P

MESH = pl.DeviceIdType.MESH
F32 = jnp.float32
BF16 = jnp.bfloat16
TILE = 128


def send(src, dst, send_sem, recv_sem, where):
    copy = pltpu.make_async_remote_copy(
        src_ref=src, dst_ref=dst, send_sem=send_sem, recv_sem=recv_sem,
        device_id=where, device_id_type=MESH,
    )
    copy.start()
    return copy


def greet(places):
    barrier = pltpu.get_barrier_semaphore()
    for place in places:
        pl.semaphore_signal(barrier, inc=1, device_id=place, device_id_type=MESH)
    pl.semaphore_wait(barrier, len(places))


def dot(a, b, dims):
    return lax.dot_general(a, b, (dims, ((), ())), preferred_element_type=F32)


class Place:
    def __init__(self, bands, groups):
        self.bands = bands
        self.me = lax.axis_index("band")
        ga = lax.axis_index("ga")
        self.core = lax.rem(ga, 2)
        self.row = lax.rem(ga // 2, 2)
        self.partner = {"ga": ga + 1 - 2 * self.core}
        self.across = {"ga": ga + 2 - 4 * self.row}
        self.peer = [lax.rem(self.me + d, bands) for d in range(bands)]
        self.far = sorted(range(1, bands), key=lambda d: -min(d, bands - d))
        self.near = self.far[::-1]
        self.bits = []
        stride = 4
        while stride < groups:
            self.bits.append({"ga": ga + stride * (1 - 2 * lax.rem(ga // stride, 2))})
            stride *= 2

    def band(self, d):
        return {"band": self.peer[d]}

    def everyone(self):
        return [self.band(d) for d in range(1, self.bands)] + [self.partner, self.across] + self.bits


def span(index, size, offset=0):
    return pl.ds(pl.multiple_of(offset + index * size, 16), size)


def reduce_scratch(rows, bands, levels):
    h1, h2 = rows // 2, rows // 4
    h3 = h2 // bands
    dma = pltpu.SemaphoreType.DMA
    shapes = [
        ((rows, TILE), F32), ((rows, TILE), BF16), ((h1, TILE), BF16),
        ((h1, TILE), F32), ((h1, TILE), BF16), ((h2, TILE), BF16),
        ((h2, TILE), F32), ((h2, TILE), BF16), ((bands, h3, TILE), BF16),
        ((levels, h3, TILE), BF16), ((levels, h3, TILE), BF16), ((rows, TILE), BF16),
    ]
    return [pltpu.VMEM(*shape) for shape in shapes] + [
        dma((4,)), dma((bands,)), dma((bands,)), dma((levels,)), dma((levels,)),
        dma((bands,)), dma((bands,)), dma((bands,)), dma((bands,)),
        dma((2 * bands,)), dma((2 * bands,)),
    ]


def reduce_stages(at, scratch):
    (p32, p16, rx1, a32, a16, rx2, b32, b16, rx3, out_x, rx_x, allg,
     one, z_s, z_r, x_s, x_r, g_s, g_r, y_s, y_r, f_s, f_r) = scratch
    h1, h2 = rx1.shape[0], rx2.shape[0]
    h3 = h2 // at.bands
    copy = send(p16.at[span(1 - at.core, h1)], rx1, one.at[0], one.at[1], at.partner)
    yield
    copy.wait()
    a32[...] = p32[span(at.core, h1), :] + rx1[...].astype(F32)
    a16[...] = a32[...].astype(BF16)
    copy = send(a16.at[span(1 - at.row, h2)], rx2, one.at[2], one.at[3], at.across)
    yield
    copy.wait()
    b32[...] = a32[span(at.row, h2), :] + rx2[...].astype(F32)
    b16[...] = b32[...].astype(BF16)
    copies = [send(b16.at[span(at.peer[d], h3)], rx3.at[d], z_s.at[d], z_r.at[d], at.band(d))
              for d in at.far]
    yield
    for copy in copies:
        copy.wait()
    total = b32[span(at.me, h3), :]
    for d in range(1, at.bands):
        total = total + rx3[d].astype(F32)
    for i, place in enumerate(at.bits):
        out_x[i] = total.astype(BF16)
        send(out_x.at[i], rx_x.at[i], x_s.at[i], x_r.at[i], place).wait()
        total = out_x[i].astype(F32) + rx_x[i].astype(F32)

    def piece(d, row):
        source = lax.rem(at.me + at.bands - d, at.bands)
        return allg.at[span(source, h3, at.core * h1 + row * h2)]

    allg[span(at.me, h3, at.core * h1 + at.row * h2), :] = total.astype(BF16)
    own = piece(0, at.row)
    gathers = {d: send(own, own, g_s.at[d], g_r.at[d], at.band(d)) for d in at.far}
    sides = {0: send(own, own, y_s.at[0], y_r.at[0], at.across)}
    lasts = [send(own, own, f_s.at[0], f_r.at[0], at.partner)]
    yield
    for d in at.near:
        gathers[d].wait()
        there = piece(d, at.row)
        sides[d] = send(there, there, y_s.at[d], y_r.at[d], at.across)
        lasts.append(send(there, there, f_s.at[d], f_r.at[d], at.partner))
    yield
    for d in [0] + at.near:
        sides[d].wait()
        there = piece(d, 1 - at.row)
        e = at.bands + d
        lasts.append(send(there, there, f_s.at[e], f_r.at[e], at.partner))
    yield
    for copy in lasts:
        copy.wait()


def margin_kernel(bands, groups, orb, kern, m_out, w_out, full, loc, a_s, a_r, *scratch):
    at = Place(bands, groups)
    own = orb.shape[0]
    cols = orb.shape[1] // bands
    n = own * bands
    greet(at.everyone())

    def chunk(d):
        return pl.ds(pl.multiple_of(at.peer[d] * cols, TILE), cols)

    mine = full.at[span(at.me, own)]
    local = pltpu.make_async_copy(orb.at[:, chunk(0)], mine, loc.at[0])
    local.start()
    copies = [send(orb.at[:, chunk(d)], mine, a_s.at[d], a_r.at[d], at.band(d)) for d in at.far]
    local.wait()
    for copy in copies:
        copy.wait()
    w_out[...] = (-(full[...].astype(F32) * kern[:, chunk(0)])).astype(BF16)
    p32, p16, allg = scratch[0], scratch[1], scratch[11]
    row = 0
    for s in range(0, n, TILE):
        e = s + TILE
        product = dot(w_out[s:e, :], full[0:e, :], ((1,), (1,)))
        for c in range(0, e, TILE):
            p32[row:row + TILE, :] = product[:, c:c + TILE]
            p16[row:row + TILE, :] = product[:, c:c + TILE].astype(BF16)
            row += TILE
    if row < p32.shape[0]:
        p32[row:, :] = jnp.zeros((p32.shape[0] - row, TILE), F32)
        p16[row:, :] = jnp.zeros((p32.shape[0] - row, TILE), BF16)
    for _ in reduce_stages(at, scratch):
        pass
    m_out[...] = allg[...]


def split(a):
    high = a.astype(BF16)
    return high, (a - high.astype(F32)).astype(BF16)


def product3(a, b, dims):
    (ah, al), (bh, bl) = split(a), split(b)
    return dot(ah, bh, dims) + (dot(ah, bl, dims) + dot(al, bh, dims))


def identity(rows):
    shape = (rows, rows)
    return (lax.broadcasted_iota(jnp.int32, shape, 0)
            == lax.broadcasted_iota(jnp.int32, shape, 1)).astype(F32)


def factor_tile(d_ref, t_ref):
    G = 8
    sub = lax.broadcasted_iota(jnp.int32, (G, TILE), 0)

    def spread(row):
        return jnp.broadcast_to(row, (G, TILE))

    def step(g, carry):
        start = pl.multiple_of(g * G, G)
        left = d_ref[pl.ds(start, G), 0:TILE]
        right = d_ref[pl.ds(start, G), TILE:2 * TILE]
        turned = pltpu.roll(left, lax.rem(TILE - start, TILE), 1)
        columns = [jnp.broadcast_to(turned[:, c:c + 1], (G, TILE)) for c in range(G)]
        d = [[spread(columns[c][i:i + 1, :]) for c in range(i + 1)] for i in range(G)]
        u, v = [], []
        u_all = v_all = jnp.zeros((G, TILE), F32)
        for j in range(G):
            r = lax.rsqrt(d[j][j])
            for i in range(j + 1, G):
                d[i][j] = d[i][j] * r
            for i in range(j + 1, G):
                for c in range(j + 1, i + 1):
                    d[i][c] = d[i][c] - d[i][j] * d[c][j]
            a, b = spread(left[j:j + 1, :]), spread(right[j:j + 1, :])
            for t in range(j):
                a = a - d[j][t] * u[t]
                b = b - d[j][t] * v[t]
            u.append(a * r)
            v.append(b * r)
            u_all = jnp.where(sub == j, u[j], u_all)
            v_all = jnp.where(sub == j, v[j], v_all)
        t_ref[pl.ds(start, G), :] = v_all
        both = jnp.concatenate([u_all, v_all], axis=1)
        high = both.astype(BF16).astype(F32)
        low = both - high
        lhs = jnp.concatenate([high[:, :TILE], high[:, :TILE], low[:, :TILE], low[:, :TILE]], axis=0)
        rhs = jnp.concatenate([high, low, high, low], axis=0)
        d_ref[...] -= dot(lhs.astype(BF16), rhs.astype(BF16), ((0,), (0,)))
        return carry

    lax.fori_loop(0, TILE // G, step, 0)


def apply_kernel(bands, groups, m_ref, w, blk, ace, exch, a, rest, d_ref, t_ref, x16, proj,
                 bfull, applied, loc, b_s, b_r, p_s, p_r, e_s, e_r, *scratch):
    at = Place(bands, groups)
    me = at.me
    own, bown = ace.shape[0], exch.shape[0]
    cols = w.shape[1]
    n, nblk = own * bands, bown * bands
    scale = 1.0 / (ace.shape[1] * groups)
    greet(at.everyone())

    def chunk(index):
        return pl.ds(pl.multiple_of(index * cols, TILE), cols)

    mine = bfull.at[span(me, bown)]
    local = pltpu.make_async_copy(blk.at[:, chunk(me)], mine, loc.at[0])
    local.start()
    blocks = [send(blk.at[:, chunk(at.peer[d])], mine, b_s.at[d], b_r.at[d], at.band(d))
              for d in at.far]
    row = 0
    for s in range(0, n, TILE):
        for c in range(0, s + TILE, TILE):
            a[s:s + TILE, c:c + TILE] = m_ref[row:row + TILE, :].astype(F32) * -scale
            row += TILE
    rest[...] = identity(n)
    x16[...] = jnp.zeros_like(x16)
    p32, p16, allg = scratch[0], scratch[1], scratch[11]

    def stages():
        local.wait()
        for copy in blocks:
            copy.wait()
        half = nblk // 2
        for h in range(2):
            product = dot(w[...], bfull[h * half:(h + 1) * half, :], ((1,), (1,)))
            p32[h * n:(h + 1) * n, :] = product
            p16[h * n:(h + 1) * n, :] = product.astype(BF16)
        yield from reduce_stages(at, scratch)

    cuts = sorted(set(range(0, n, TILE)) | set(range(0, n, own)) | {n})
    pieces = list(enumerate(zip(cuts[:-1], cuts[1:])))

    def piece(q, r0, r1, source, target):
        lo = r0 % own
        return pltpu.make_async_remote_copy(
            src_ref=proj.at[r0:r1], dst_ref=ace.at[lo:lo + r1 - r0, chunk(source)],
            send_sem=p_s.at[q], recv_sem=p_r.at[q, source],
            device_id={"band": target}, device_id_type=MESH)

    def kept(q, r0, r1):
        lo = r0 % own
        return pltpu.make_async_copy(
            proj.at[r0:r1], ace.at[lo:lo + r1 - r0, chunk(me)], p_s.at[q])

    steps = stages()
    for s in range(0, n, TILE):
        e = s + TILE
        d_ref[:, 0:TILE] = a[s:e, s:e]
        d_ref[:, TILE:] = identity(TILE)
        factor_tile(d_ref, t_ref)
        tile = t_ref[...]
        rows = product3(tile, rest[s:e, 0:e], ((1,), (0,)))
        high, low = split(rows)
        x16[s:e, 0:e] = high
        proj[s:e, :] = (dot(high, w[0:e, :], ((1,), (0,)))
                        + dot(low, w[0:e, :], ((1,), (0,)))).astype(BF16)
        for q, (r0, r1) in pieces:
            if s <= r0 < e:
                owner = r0 // own

                @pl.when(me != owner)
                def _():
                    piece(q, r0, r1, me, owner).start()

                @pl.when(me == owner)
                def _():
                    kept(q, r0, r1).start()
        if e < n:
            panel = product3(a[e:, s:e], tile, ((1,), (1,)))
            for c in range(e, n, TILE):
                a[c:, c:c + TILE] -= product3(panel[c - e:], panel[c - e:c - s], ((1,), (1,)))
            rest[e:, 0:e] -= product3(panel, rows, ((1,), (0,)))
        next(steps, None)
    for _ in steps:
        pass
    half = nblk // 2
    for h in range(2):
        coupling = dot(x16[...], allg[h * n:(h + 1) * n, :], ((1,), (0,))) * scale
        applied[h * half:(h + 1) * half, :] = (
            -dot(coupling.astype(BF16), proj[...], ((0,), (0,)))).astype(BF16)
    outs = [send(applied.at[span(at.peer[d], bown)], exch.at[:, chunk(me)],
                 e_s.at[d], e_r.at[d], at.band(d)) for d in at.far]
    outs.append(pltpu.make_async_copy(applied.at[span(me, bown)], exch.at[:, chunk(me)], loc.at[1]))
    outs[-1].start()
    for q, (r0, r1) in pieces:
        owner = r0 // own

        @pl.when(me != owner)
        def _():
            piece(q, r0, r1, me, owner).wait_send()

        @pl.when(me == owner)
        def _():
            kept(q, r0, r1).wait()
            for d in range(1, bands):
                piece(q, r0, r1, at.peer[d], at.peer[d]).wait_recv()
    for copy in outs:
        copy.wait()


def shards(orbitals, kernel, block_vectors):
    groups, bands = lax.axis_size("ga"), lax.axis_size("band")
    own, width = orbitals.shape
    bown = block_vectors.shape[0]
    cols = width // bands
    n, nblk = own * bands, bown * bands
    levels = max(groups.bit_length() - 3, 1)
    unit = 4 * bands * 16
    tiles = n // TILE
    flat = -(-(tiles * (tiles + 1) // 2 * TILE) // unit) * unit
    pieces = len(set(range(0, n, TILE)) | set(range(0, n, own)))
    vmem, hbm = pl.BlockSpec(memory_space=pltpu.VMEM), pl.BlockSpec(memory_space=pl.ANY)
    dma = pltpu.SemaphoreType.DMA
    many = dma((bands,))
    margin, weighted = pl.pallas_call(
        functools.partial(margin_kernel, bands, groups),
        name="margin",
        out_shape=(
            jax.ShapeDtypeStruct((flat, TILE), BF16),
            jax.ShapeDtypeStruct((n, cols), BF16),
        ),
        in_specs=[hbm, vmem],
        out_specs=(vmem, vmem),
        scratch_shapes=[pltpu.VMEM((n, cols), BF16), dma((1,)), many, many]
        + reduce_scratch(flat, bands, levels),
        compiler_params=pltpu.CompilerParams(
            collective_id=0, has_side_effects=True, vmem_limit_bytes=48 * 2**20),
    )(orbitals, kernel.reshape(1, width))
    return pl.pallas_call(
        functools.partial(apply_kernel, bands, groups),
        name="apply",
        out_shape=(
            jax.ShapeDtypeStruct((own, width), BF16),
            jax.ShapeDtypeStruct((bown, width), BF16),
        ),
        in_specs=[vmem, vmem, hbm],
        out_specs=(hbm, hbm),
        scratch_shapes=[
            pltpu.VMEM((n, n), F32),
            pltpu.VMEM((n, n), F32),
            pltpu.VMEM((TILE, 2 * TILE), F32),
            pltpu.VMEM((TILE, TILE), F32),
            pltpu.VMEM((n, n), BF16),
            pltpu.VMEM((n, cols), BF16),
            pltpu.VMEM((nblk, cols), BF16),
            pltpu.VMEM((nblk, cols), BF16),
            dma((2,)), many, many, dma((pieces,)), dma((pieces, bands)), many, many,
        ] + reduce_scratch(2 * n, bands, levels),
        compiler_params=pltpu.CompilerParams(
            collective_id=1, has_side_effects=True, vmem_limit_bytes=48 * 2**20),
    )(margin, weighted, block_vectors)


def solution(mesh):
    placed = (P(("img", "band"), "ga"), P("ga"), P(("img", "band"), "ga"))
    return jax.shard_map(
        shards,
        mesh=mesh,
        in_specs=placed,
        out_specs=(P(("img", "band"), "ga"), P(("img", "band"), "ga")),
        check_vma=False,
    )
```

time: 553 us -> 135 us (0.24); the launches traced: 546 us -> 135 us
  waiting for transfers between devices: 262 us -> 0 us
  other arithmetic: 195 us -> 0 us
  Pallas kernels: 0 us -> 131 us
  matrix products: 41.5 us -> 0 us
  local copies, waits for them, and re-layouts: 28.5 us -> 3.73 us
  between operations: 18.6 us -> 0.66 us
    another operation x25 -> x0, other arithmetic: 186 us -> none  [the longest x22 124 us: shards(): factor = jnp.linalg.cholesky(margin)]
    all_gather x3 -> x0, waiting for transfers between devices: 137 us -> none  [the longest x1 89.3 us: shards(): lax.all_gather(orbitals, 'band', axis=0, tiled=True)]
    pallas_call x0 -> x2, Pallas kernels: none -> 131 us  [the longest x1 79.1 us: shards(): pl.pallas_call(functools.partial(apply_kernel, bands, groups), name='appl...]
    psum x2 -> x0, waiting for transfers between devices: 63.7 us -> none  [the longest x1 32.5 us: shards(): lax.psum(partial_rows.astype(jnp.bfloat16), 'ga').astype(jnp.float32)]
    reduce_scatter x1 -> x0, waiting for transfers between devices: 60.5 us -> none  [shards(): lax.psum_scatter(-contract_first(coupling, projector), 'band', scatter_di...]
    another operation x21 -> x0, matrix products: 23 us -> none  [the longest x11 13.2 us: shards(): lax.linalg.triangular_solve(factor, identity, left_side=True, lower=True)]
    another operation x25 -> x0, local copies, waits for them, and re-layouts: 21.5 us -> none
    dot_general x4 -> x0, matrix products: 18.5 us -> none  [the longest x1 5.31 us: contract_first(): lax.dot_general(left, right, (((0,), (0,)), ((), ())), precision=lax.Prec...]
  transfers between devices with their start and end apart: 6 -> 0, of which waited for: 5 -> 0; matrix products, arithmetic and copies ran while one was open for 45% -> 0% of each run, Pallas kernels for 0% -> 0%
where the time goes in v2:
time: 135 us
  Pallas kernels  131 us (97%)
  local copies, waits for them, and re-layouts  3.73 us (3%)
    pallas_call x1, Pallas kernels, shards(): pl.pallas_call(functools.partial(apply_kernel, bands, groups), name='appl...  79.1 us
    pallas_call x1, Pallas kernels, shards(): pl.pallas_call(functools.partial(margin_kernel, bands, groups), name='mar...  51.7 us
    unnamed x8, local copies, waits for them, and re-layouts  3.73 us

profile of v2, /device:TPU:25, one launch (start us, length us, event | category | flops | bytes accessed | tf_op | source)
XLA Modules:
  0.0 135.2 jit_solution(17213540424240160641)
XLA Ops:
  0.6 0.0 copy-start
  0.6 1.3 copy-done
  1.9 0.0 copy-start.2
  1.9 0.7 copy-done.2
  2.6 0.0 copy-start.1
  2.6 51.7 %margin.1 = (bf16[2816,128]{1,0:T(8,128)(2,1)S(1)}, bf16[768,768]{1,0:T(8,128)(2,1)S(1)}) custom-call(bf16[192,3072]{1,0:T(8,128)(2,1)S(1)} %copy-done, f32[1,3072]{1,0:T(1,128)S(1)} %bitcast.1), custom_call_target="tpu_custom_call" | custom-call | tf_op jit(solution)/shard_map/margin/pallas_call | solution.py:353
  54.3 0.0 copy-done.1
  54.3 79.1 %apply.1 = (bf16[192,3072]{1,0:T(8,128)(2,1)S(1)}, bf16[64,3072]{1,0:T(8,128)(2,1)S(1)}) custom-call(bf16[2816,128]{1,0:T(8,128)(2,1)S(1)} %get-tuple-element.4.m_ref, bf16[768,768]{1,0:T(8,128)(2,1)S(1)} %get-tuple-element.5.w, bf16[64,3072]{1,0:T(8,128)(2,1)S(1)} %copy-done.1), custom_call_target="tpu_custom_call" | custom-call | tf_op jit(solution)/shard_map/apply/pallas_call | solution.py:367
  133.4 1.0 copy.7
  134.4 0.7 copy.8
Async XLA Ops:
  0.6 1.3 copy-start
  1.9 0.7 copy-start.2
  2.6 51.7 %copy-start.1 = (bf16[64,3072]{1,0:T(8,128)(2,1)S(1)}, bf16[64,3072]{1,0:T(8,128)(2,1)}, u32[]{:S(2)}) copy-start(bf16[64,3072]{1,0:T(8,128)(2,1)} %blk.1) | copy-start | bytes 1179652

commit v3 on v2

--- a/solution.py
+++ b/solution.py
@@ -185,42 +185,63 @@
 
 
 def factor_tile(d_ref, t_ref):
-    G = 8
-    sub = lax.broadcasted_iota(jnp.int32, (G, TILE), 0)
-
-    def spread(row):
-        return jnp.broadcast_to(row, (G, TILE))
+    G, SUB = 32, 8
+    H = G // SUB
+    sub = lax.broadcasted_iota(jnp.int32, (SUB, TILE), 0)
+
+    def spread(block, i):
+        return jnp.broadcast_to(block[i:i + 1, :], (SUB, TILE))
+
+    def lane(block, c):
+        return jnp.broadcast_to(block[:, c:c + 1], (SUB, TILE))
 
     def step(g, carry):
         start = pl.multiple_of(g * G, G)
-        left = d_ref[pl.ds(start, G), 0:TILE]
+        turned = pltpu.roll(d_ref[pl.ds(start, G), 0:TILE], lax.rem(TILE - start, TILE), 1)
         right = d_ref[pl.ds(start, G), TILE:2 * TILE]
-        turned = pltpu.roll(left, lax.rem(TILE - start, TILE), 1)
-        columns = [jnp.broadcast_to(turned[:, c:c + 1], (G, TILE)) for c in range(G)]
-        d = [[spread(columns[c][i:i + 1, :]) for c in range(i + 1)] for i in range(G)]
-        u, v = [], []
-        u_all = v_all = jnp.zeros((G, TILE), F32)
-        for j in range(G):
-            r = lax.rsqrt(d[j][j])
-            for i in range(j + 1, G):
-                d[i][j] = d[i][j] * r
-            for i in range(j + 1, G):
-                for c in range(j + 1, i + 1):
-                    d[i][c] = d[i][c] - d[i][j] * d[c][j]
-            a, b = spread(left[j:j + 1, :]), spread(right[j:j + 1, :])
-            for t in range(j):
-                a = a - d[j][t] * u[t]
-                b = b - d[j][t] * v[t]
-            u.append(a * r)
-            v.append(b * r)
-            u_all = jnp.where(sub == j, u[j], u_all)
-            v_all = jnp.where(sub == j, v[j], v_all)
+        lefts = [turned[h * SUB:(h + 1) * SUB, :] for h in range(H)]
+        rights = [right[h * SUB:(h + 1) * SUB, :] for h in range(H)]
+        us, vs = [], []
+        for b in range(H):
+            columns = [lane(lefts[b], b * SUB + c) for c in range(SUB)]
+            d = [[spread(columns[c], i) for c in range(i + 1)] for i in range(SUB)]
+            below = {h: [lane(lefts[h], b * SUB + c) for c in range(SUB)] for h in range(b + 1, H)}
+            u, v = [], []
+            u_all = v_all = jnp.zeros((SUB, TILE), F32)
+            for j in range(SUB):
+                r = lax.rsqrt(d[j][j])
+                for i in range(j + 1, SUB):
+                    d[i][j] = d[i][j] * r
+                for i in range(j + 1, SUB):
+                    for c in range(j + 1, i + 1):
+                        d[i][c] = d[i][c] - d[i][j] * d[c][j]
+                p, q = spread(lefts[b], j), spread(rights[b], j)
+                for t in range(j):
+                    p = p - d[j][t] * u[t]
+                    q = q - d[j][t] * v[t]
+                u.append(p * r)
+                v.append(q * r)
+                u_all = jnp.where(sub == j, u[j], u_all)
+                v_all = jnp.where(sub == j, v[j], v_all)
+                for h in range(b + 1, H):
+                    n = below[h][j]
+                    for t in range(j):
+                        n = n - below[h][t] * d[j][t]
+                    below[h][j] = n * r
+            us.append(u_all)
+            vs.append(v_all)
+            for h in range(b + 1, H):
+                for j in range(SUB):
+                    lefts[h] = lefts[h] - below[h][j] * u[j]
+                    rights[h] = rights[h] - below[h][j] * v[j]
+        u_all = pltpu.roll(jnp.concatenate(us, axis=0), start, 1)
+        v_all = jnp.concatenate(vs, axis=0)
         t_ref[pl.ds(start, G), :] = v_all
         both = jnp.concatenate([u_all, v_all], axis=1)
         high = both.astype(BF16).astype(F32)
         low = both - high
-        lhs = jnp.concatenate([high[:, :TILE], high[:, :TILE], low[:, :TILE], low[:, :TILE]], axis=0)
-        rhs = jnp.concatenate([high, low, high, low], axis=0)
+        lhs = jnp.concatenate([high[:, :TILE], high[:, :TILE], low[:, :TILE]], axis=0)
+        rhs = jnp.concatenate([high, low, high], axis=0)
         d_ref[...] -= dot(lhs.astype(BF16), rhs.astype(BF16), ((0,), (0,)))
         return carry
 

time: 135 us -> 130 us (0.963); the launches traced: 135 us -> 128 us
  Pallas kernels: 131 us -> 124 us
    pallas_call x1, Pallas kernels: 79.1 us -> 72.4 us  [shards(): pl.pallas_call(functools.partial(apply_kernel, bands, groups), name='appl...]
where the time goes in v3:
time: 130 us; the launch traced here: 128 us
  Pallas kernels  124 us (95%)
  local copies, waits for them, and re-layouts  3.73 us (3%)
    pallas_call x1, Pallas kernels, shards(): pl.pallas_call(functools.partial(apply_kernel, bands, groups), name='appl...  72.4 us
    pallas_call x1, Pallas kernels, shards(): pl.pallas_call(functools.partial(margin_kernel, bands, groups), name='mar...  51.7 us
    unnamed x8, local copies, waits for them, and re-layouts  3.73 us

profile of v3, /device:TPU:25, one launch (start us, length us, event | category | flops | bytes accessed | tf_op | source)
XLA Modules:
  0.0 128.5 jit_solution(11724149395631361736)
XLA Ops:
  0.6 0.0 copy-start
  0.6 1.3 copy-done
  1.9 0.0 copy-start.2
  1.9 0.7 copy-done.2
  2.6 0.0 copy-start.1
  2.6 51.7 %margin.1 = (bf16[2816,128]{1,0:T(8,128)(2,1)S(1)}, bf16[768,768]{1,0:T(8,128)(2,1)S(1)}) custom-call(bf16[192,3072]{1,0:T(8,128)(2,1)S(1)} %copy-done, f32[1,3072]{1,0:T(1,128)S(1)} %bitcast.1), custom_call_target="tpu_custom_call" | custom-call | tf_op jit(solution)/shard_map/margin/pallas_call | solution.py:374
  54.3 0.0 copy-done.1
  54.3 72.4 %apply.1 = (bf16[192,3072]{1,0:T(8,128)(2,1)S(1)}, bf16[64,3072]{1,0:T(8,128)(2,1)S(1)}) custom-call(bf16[2816,128]{1,0:T(8,128)(2,1)S(1)} %get-tuple-element.4.m_ref, bf16[768,768]{1,0:T(8,128)(2,1)S(1)} %get-tuple-element.5.w, bf16[64,3072]{1,0:T(8,128)(2,1)S(1)} %copy-done.1), custom_call_target="tpu_custom_call" | custom-call | tf_op jit(solution)/shard_map/apply/pallas_call | solution.py:388
  126.7 1.0 copy.7
  127.7 0.7 copy.8
Async XLA Ops:
  0.6 1.3 copy-start
  1.9 0.7 copy-start.2
  2.6 51.7 %copy-start.1 = (bf16[64,3072]{1,0:T(8,128)(2,1)S(1)}, bf16[64,3072]{1,0:T(8,128)(2,1)}, u32[]{:S(2)}) copy-start(bf16[64,3072]{1,0:T(8,128)(2,1)} %blk.1) | copy-start | bytes 1179652
